TPU v7x, 32 devices: a whole 2x2x4 slice. The times are simulated.
32 devices in a mesh: parts: 2 (over y), rows: 4 (over x, core), cols: 4 (over z).
Axes of the slice: x: 2, y: 2, z: 4, core: 2. Of those that a mesh axis runs over, the one named last changes fastest.
Arguments:
- singles: bfloat16 [1024, 384], P(('parts', 'rows', 'cols')), parts along dimension 0, may hold values from -120 to 120
- pair: bfloat16 [1024, 512, 128], P(('parts', 'rows'), 'cols'), parts along dimension 0, may hold values from -6 to 6
- chain_sizes: int32 [16], P('parts'), parts along dimension 0, may hold values from 1 to 128, 512 in all
- single_proj: bfloat16 [384, 1536], replicated, may hold values from -1 to 1
- query_bias: float32 [384], replicated, may hold values from -5 to 5
- pair_proj: bfloat16 [128, 16], replicated, may hold values from -0.5 to 0.5
- out_proj: bfloat16 [384, 384], replicated, may hold values from -1.25 to 1.25
Outputs:
- update: bfloat16 [1024, 384], P(('parts', 'rows', 'cols')), parts along dimension 0
There are 2 independent parts, one for each index of `parts`. A program takes and returns all parts, laid end to end along the dimension named above; an argument that names none is the same for every part. Nothing has to cross between parts.
Inputs may be any that keep to these rules, and one draw needn't show every extreme that they name: `chain_sizes`: the first 7 entries count the tokens of the chains in order; the last one counts the padding tokens at the end of the complex.
All inputs are finite; a program needn't handle non-finite values.
Results may differ from a plain program's by a relative error of at most 0.004.
The roundings to bfloat16 on the way count: a program that leaves them out, or rounds other values in their place, can miss the bound.
Values may be sent and summed in bfloat16 or wider, within the bound.
A program may use at most 64 MiB of HBM per device.

v0:
```python
import math

import jax
import jax.numpy as jnp
from jax import lax
from jax.sharding import PartitionSpec as P


def normalize(matrix):
    average = jnp.mean(matrix, axis=-1, keepdims=True)
    centered = matrix - average
    variance = jnp.mean(centered * centered, axis=-1, keepdims=True)
    return centered * lax.rsqrt(variance + 1e-05)


def tile_bias(pair, pair_proj):
    tile_rows, tile_cols, channels = pair.shape
    head_count = pair_proj.shape[1]
    row_block = math.gcd(tile_rows, 32)
    blocks = pair.reshape(tile_rows // row_block, row_block, tile_cols, channels)

    def project(pair_rows):
        pair_normed = normalize(pair_rows.astype(jnp.float32)).astype(jnp.bfloat16)
        return jnp.einsum(
            "ikc,ch->hik", pair_normed, pair_proj, preferred_element_type=jnp.float32
        ).astype(jnp.bfloat16)

    stacked = lax.map(project, blocks)
    return jnp.moveaxis(stacked, 1, 0).reshape(head_count, tile_rows, tile_cols)


def shards(singles, pair, chain_sizes, single_proj, query_bias, pair_proj, out_proj):
    own_rows, features = singles.shape
    head_count = pair_proj.shape[1]
    head_dim = features // head_count
    score_scale = head_dim ** (-0.5)
    normed = normalize(singles.astype(jnp.float32)).astype(jnp.bfloat16)
    projected = jnp.dot(normed, single_proj, preferred_element_type=jnp.float32)
    queries = (projected[:, :features] + query_bias).astype(jnp.bfloat16)
    key_rows = projected[:, features : 2 * features].astype(jnp.bfloat16)
    values = projected[:, 2 * features : 3 * features].astype(jnp.bfloat16)
    gating = jax.nn.sigmoid(projected[:, 3 * features :])
    live_count = jnp.sum(chain_sizes[:-1])
    bias_tile = tile_bias(pair, pair_proj)
    key_value = jnp.concatenate([key_rows, values], axis=1)
    gathered = lax.all_gather(key_value, ("rows", "cols"), axis=0, tiled=True)
    bias_own = lax.all_to_all(bias_tile, "cols", split_axis=1, concat_axis=2, tiled=True)
    key_count = gathered.shape[0]
    key_heads = gathered[:, :features].reshape(key_count, head_count, head_dim)
    value_heads = gathered[:, features:].reshape(key_count, head_count, head_dim)
    query_heads = queries.reshape(own_rows, head_count, head_dim)
    scores = jnp.einsum(
        "qhd,khd->hqk", query_heads, key_heads, preferred_element_type=jnp.float32
    ) * score_scale + bias_own.astype(jnp.float32)
    key_live = jnp.arange(key_count, dtype=jnp.int32) < live_count
    scores = jnp.where(key_live[None, None, :], scores, -1e30)
    maxima = jnp.max(scores, axis=-1, keepdims=True)
    weights = jnp.exp(scores - maxima)
    totals = jnp.sum(weights, axis=-1)
    numerator = jnp.einsum(
        "hqk,khd->qhd",
        weights.astype(jnp.bfloat16),
        value_heads,
        preferred_element_type=jnp.float32,
    )
    averaged = (numerator / jnp.transpose(totals)[:, :, None]).reshape(own_rows, features)
    attended = (gating * averaged).astype(jnp.bfloat16)
    return jnp.dot(attended, out_proj, preferred_element_type=jnp.float32).astype(jnp.bfloat16)


def solution(mesh):
    placed = (
        P(("parts", "rows", "cols"), None),
        P(("parts", "rows"), "cols", None),
        P("parts"),
        P(),
        P(),
        P(),
        P(),
    )
    return jax.shard_map(
        shards,
        mesh=mesh,
        in_specs=placed,
        out_specs=P(("parts", "rows", "cols"), None),
        check_vma=False,
    )
```

profile of v0, /device:TPU:0, one launch (start us, length us, event | category | flops | bytes accessed | tf_op | source)
XLA Modules:
  0.0 86.1 jit_solution(3081833499026486826)
XLA Ops:
  0.0 0.0 copy-start
  0.0 0.0 copy-start.2
  0.0 28.6 %while.10 = (s32[]{:T(128)}, bf16[4,16,32,128]{3,1,2,0:T(8,128)(2,1)}, bf16[4,32,128,128]{3,2,1,0:T(8,128)(2,1)}, bf16[128,16]{0,1:T(8,128)(2,1)}, s32[]{:T(128)}) while((s32[]{:T(128)}, bf16[4,16,32,128]{3,1,2,0:T(8,128)(2,1)}, bf16[4,32,128,128]{3,2,1,0:T(8,128)(2,1)}, bf16[128,16]{0,1:T(8,128)(2,1)}, s32[]{:T(128)}) %tuple.23), condition=%wide.region_6.7_spmd, body=%wide.region_3.6_spmd.sunk | while | flops 22089728 | bytes 3445865 | solution.py:28
  0.0 0.0 copy-start.4
  0.0 1.7 %convert_reduce_fusion.3 = f32[32,128]{1,0:T(8,128)S(1)} fusion(bf16[4,32,128,128]{3,2,1,0:T(8,128)(2,1)} %get-tuple-element.77, s32[]{:T(128)S(6)} %copy.31), kind=kLoop, calls=%fused_computation.clone.1 | loop fusion | flops 1044480 | bytes 1064964 | tf_op jit(solution)/shard_map/while/body/eval_jaxpr/reduce_sum | solution.py:10
  1.7 2.3 %fusion.50 = f32[32,128]{1,0:T(8,128)S(1)} fusion(f32[32,128]{1,0:T(8,128)S(1)} %broadcast_multiply_fusion.3, bf16[4,32,128,128]{3,2,1,0:T(8,128)(2,1)} %get-tuple-element.77, s32[]{:T(128)S(6)} %copy.31), kind=kLoop, calls=%fused_computation.5.clone.1 | loop fusion | flops 2093056 | bytes 1081348 | tf_op jit(solution)/shard_map/while/body/eval_jaxpr/reduce_sum | solution.py:12
  4.1 0.0 copy-done.4
  4.1 3.1 %fusion.51 = bf16[4,16,32,128]{3,1,2,0:T(8,128)(2,1)} fusion(bf16[4,16,32,128]{3,1,2,0:T(8,128)(2,1)} %get-tuple-element.71, s32[]{:T(128)S(6)} %copy.31, f32[32,128]{1,0:T(8,128)S(1)} %add_rsqrt_fusion.3, f32[32,128]{1,0:T(8,128)S(1)} %broadcast_multiply_fusion.3, bf16[4,32,128,128]{3,2,1,0:T(8,128)(2,1)} %get-tuple-element.77, ...), kind=kOutput, calls=%fused_computation.9.clone.1 | convolution fusion | flops 18939904 | bytes 1217536 | tf_op jit(solution)/shard_map/while/body/eval_jaxpr/ikc,ch->hik/dot_general | solution.py:24
  7.2 0.0 copy-start.4
  7.2 1.6 %convert_reduce_fusion.3 = f32[32,128]{1,0:T(8,128)S(1)} fusion(bf16[4,32,128,128]{3,2,1,0:T(8,128)(2,1)} %get-tuple-element.77, s32[]{:T(128)S(6)} %copy.31), kind=kLoop, calls=%fused_computation.clone.1 | loop fusion | flops 1044480 | bytes 1064964 | tf_op jit(solution)/shard_map/while/body/eval_jaxpr/reduce_sum | solution.py:10
  8.8 2.3 %fusion.50 = f32[32,128]{1,0:T(8,128)S(1)} fusion(f32[32,128]{1,0:T(8,128)S(1)} %broadcast_multiply_fusion.3, bf16[4,32,128,128]{3,2,1,0:T(8,128)(2,1)} %get-tuple-element.77, s32[]{:T(128)S(6)} %copy.31), kind=kLoop, calls=%fused_computation.5.clone.1 | loop fusion | flops 2093056 | bytes 1081348 | tf_op jit(solution)/shard_map/while/body/eval_jaxpr/reduce_sum | solution.py:12
  11.2 0.0 copy-done.4
  11.2 3.2 %fusion.51 = bf16[4,16,32,128]{3,1,2,0:T(8,128)(2,1)} fusion(bf16[4,16,32,128]{3,1,2,0:T(8,128)(2,1)} %get-tuple-element.71, s32[]{:T(128)S(6)} %copy.31, f32[32,128]{1,0:T(8,128)S(1)} %add_rsqrt_fusion.3, f32[32,128]{1,0:T(8,128)S(1)} %broadcast_multiply_fusion.3, bf16[4,32,128,128]{3,2,1,0:T(8,128)(2,1)} %get-tuple-element.77, ...), kind=kOutput, calls=%fused_computation.9.clone.1 | convolution fusion | flops 18939904 | bytes 1217536 | tf_op jit(solution)/shard_map/while/body/eval_jaxpr/ikc,ch->hik/dot_general | solution.py:24
  14.4 0.0 copy-start.4
  14.4 1.6 %convert_reduce_fusion.3 = f32[32,128]{1,0:T(8,128)S(1)} fusion(bf16[4,32,128,128]{3,2,1,0:T(8,128)(2,1)} %get-tuple-element.77, s32[]{:T(128)S(6)} %copy.31), kind=kLoop, calls=%fused_computation.clone.1 | loop fusion | flops 1044480 | bytes 1064964 | tf_op jit(solution)/shard_map/while/body/eval_jaxpr/reduce_sum | solution.py:10
  16.0 2.3 %fusion.50 = f32[32,128]{1,0:T(8,128)S(1)} fusion(f32[32,128]{1,0:T(8,128)S(1)} %broadcast_multiply_fusion.3, bf16[4,32,128,128]{3,2,1,0:T(8,128)(2,1)} %get-tuple-element.77, s32[]{:T(128)S(6)} %copy.31), kind=kLoop, calls=%fused_computation.5.clone.1 | loop fusion | flops 2093056 | bytes 1081348 | tf_op jit(solution)/shard_map/while/body/eval_jaxpr/reduce_sum | solution.py:12
  18.3 0.0 copy-done.4
  18.3 3.2 %fusion.51 = bf16[4,16,32,128]{3,1,2,0:T(8,128)(2,1)} fusion(bf16[4,16,32,128]{3,1,2,0:T(8,128)(2,1)} %get-tuple-element.71, s32[]{:T(128)S(6)} %copy.31, f32[32,128]{1,0:T(8,128)S(1)} %add_rsqrt_fusion.3, f32[32,128]{1,0:T(8,128)S(1)} %broadcast_multiply_fusion.3, bf16[4,32,128,128]{3,2,1,0:T(8,128)(2,1)} %get-tuple-element.77, ...), kind=kOutput, calls=%fused_computation.9.clone.1 | convolution fusion | flops 18939904 | bytes 1217536 | tf_op jit(solution)/shard_map/while/body/eval_jaxpr/ikc,ch->hik/dot_general | solution.py:24
  21.5 0.0 copy-start.4
  21.5 1.6 %convert_reduce_fusion.3 = f32[32,128]{1,0:T(8,128)S(1)} fusion(bf16[4,32,128,128]{3,2,1,0:T(8,128)(2,1)} %get-tuple-element.77, s32[]{:T(128)S(6)} %copy.31), kind=kLoop, calls=%fused_computation.clone.1 | loop fusion | flops 1044480 | bytes 1064964 | tf_op jit(solution)/shard_map/while/body/eval_jaxpr/reduce_sum | solution.py:10
  23.1 2.3 %fusion.50 = f32[32,128]{1,0:T(8,128)S(1)} fusion(f32[32,128]{1,0:T(8,128)S(1)} %broadcast_multiply_fusion.3, bf16[4,32,128,128]{3,2,1,0:T(8,128)(2,1)} %get-tuple-element.77, s32[]{:T(128)S(6)} %copy.31), kind=kLoop, calls=%fused_computation.5.clone.1 | loop fusion | flops 2093056 | bytes 1081348 | tf_op jit(solution)/shard_map/while/body/eval_jaxpr/reduce_sum | solution.py:12
  25.4 0.0 copy-done.4
  25.5 3.2 %fusion.51 = bf16[4,16,32,128]{3,1,2,0:T(8,128)(2,1)} fusion(bf16[4,16,32,128]{3,1,2,0:T(8,128)(2,1)} %get-tuple-element.71, s32[]{:T(128)S(6)} %copy.31, f32[32,128]{1,0:T(8,128)S(1)} %add_rsqrt_fusion.3, f32[32,128]{1,0:T(8,128)S(1)} %broadcast_multiply_fusion.3, bf16[4,32,128,128]{3,2,1,0:T(8,128)(2,1)} %get-tuple-element.77, ...), kind=kOutput, calls=%fused_computation.9.clone.1 | convolution fusion | flops 18939904 | bytes 1217536 | tf_op jit(solution)/shard_map/while/body/eval_jaxpr/ikc,ch->hik/dot_general | solution.py:24
  28.6 6.5 %all-to-all-start = ((bf16[16,128,128]{2,0,1:T(8,128)(2,1)}), bf16[16,128,128]{2,0,1:T(8,128)(2,1)S(1)}, u32[]{:S(2)}, u32[]{:S(2)}) async-start(bf16[16,128,128]{2,0,1:T(8,128)(2,1)} %bitcast.9), calls=%async_computation | async-start | bytes 1048576 | tf_op jit(solution)/shard_map/all_to_all | solution.py:47
  35.1 0.0 copy-done.2
  35.1 0.1 convert_reduce_fusion.1
  35.2 0.2 fusion.22
  35.4 0.0 copy-done
  35.4 0.4 fusion.31
  35.8 0.0 copy-done.3
  35.8 0.0 copy-start.5
  35.8 0.1 copy.24
  36.0 46.1 %all_gather.3 = bf16[512,768]{1,0:T(8,128)(2,1)S(1)} all-gather(bf16[32,768]{1,0:T(8,128)(2,1)S(1)} %slice.53), channel_id=1, replica_groups=mesh['parts'=2,'rows'=4,'cols'=4] {'rows','cols'}, dimensions={0}, use_global_device_ids=true | all-gather | bytes 835584 | tf_op jit(solution)/shard_map/all_gather | solution.py:46
  82.1 0.1 fusion.37
  82.2 0.2 copy.19
  82.4 0.2 copy.18
  82.6 0.0 copy-done.5
  82.6 0.6 slice_reduce_fusion
  83.2 0.6 iota_compare_fusion
  83.9 0.0 all-to-all-done
  83.9 0.1 copy.21
  84.0 0.0 copy-start.1
  84.0 0.5 fusion.38
  84.5 0.3 fusion.16
  84.8 0.3 fusion.15
  85.2 0.1 copy.25
  85.3 0.0 copy-done.1
  85.3 0.8 convolution_convert_fusion.1
  (14 shorter events, 0.1 us)
Async XLA Ops:
  0.0 35.4 %copy-start = (bf16[384,1536]{1,0:T(8,128)(2,1)S(1)}, bf16[384,1536]{1,0:T(8,128)(2,1)}, u32[]{:S(2)}) copy-start(bf16[384,1536]{1,0:T(8,128)(2,1)} %param.12) | copy-start | bytes 3538948
  0.0 35.1 %copy-start.2 = (bf16[32,384]{1,0:T(8,128)(2,1)S(1)}, bf16[32,384]{1,0:T(8,128)(2,1)}, u32[]{:S(2)}) copy-start(bf16[32,384]{1,0:T(8,128)(2,1)} %param.9) | copy-start | bytes 73732
  0.0 4.1 %copy-start.4 = (bf16[128,16]{0,1:T(8,128)(2,1)S(1)}, bf16[128,16]{0,1:T(8,128)(2,1)}, u32[]{:S(2)}) copy-start(bf16[128,16]{0,1:T(8,128)(2,1)} %get-tuple-element.78) | copy-start | bytes 12292 | tf_op jit(solution)/shard_map/while
  7.2 4.0 %copy-start.4 = (bf16[128,16]{0,1:T(8,128)(2,1)S(1)}, bf16[128,16]{0,1:T(8,128)(2,1)}, u32[]{:S(2)}) copy-start(bf16[128,16]{0,1:T(8,128)(2,1)} %get-tuple-element.78) | copy-start | bytes 12292 | tf_op jit(solution)/shard_map/while
  14.4 4.0 %copy-start.4 = (bf16[128,16]{0,1:T(8,128)(2,1)S(1)}, bf16[128,16]{0,1:T(8,128)(2,1)}, u32[]{:S(2)}) copy-start(bf16[128,16]{0,1:T(8,128)(2,1)} %get-tuple-element.78) | copy-start | bytes 12292 | tf_op jit(solution)/shard_map/while
  21.5 4.0 %copy-start.4 = (bf16[128,16]{0,1:T(8,128)(2,1)S(1)}, bf16[128,16]{0,1:T(8,128)(2,1)}, u32[]{:S(2)}) copy-start(bf16[128,16]{0,1:T(8,128)(2,1)} %get-tuple-element.78) | copy-start | bytes 12292 | tf_op jit(solution)/shard_map/while
  28.6 7.2 %copy-start.3 = (f32[384]{0:T(512)S(1)}, f32[384]{0:T(512)}, u32[]{:S(2)}) copy-start(f32[384]{0:T(512)} %param.13) | copy-start | bytes 4612
  28.6 55.3 %all-to-all-start = ((bf16[16,128,128]{2,0,1:T(8,128)(2,1)}), bf16[16,128,128]{2,0,1:T(8,128)(2,1)S(1)}, u32[]{:S(2)}, u32[]{:S(2)}) async-start(bf16[16,128,128]{2,0,1:T(8,128)(2,1)} %bitcast.9), calls=%async_computation | async-start | bytes 1048576 | tf_op jit(solution)/shard_map/all_to_all | solution.py:47
  35.8 46.8 %copy-start.5 = (s32[8]{0:T(128)S(1)}, s32[8]{0:T(128)}, u32[]{:S(2)}) copy-start(s32[8]{0:T(128)} %param.11) | copy-start | bytes 100
  84.0 1.3 %copy-start.1 = (bf16[384,384]{1,0:T(8,128)(2,1)S(1)}, bf16[384,384]{1,0:T(8,128)(2,1)}, u32[]{:S(2)}) copy-start(bf16[384,384]{1,0:T(8,128)(2,1)} %param.15) | copy-start | bytes 884740
where the time goes:
time: 86.6 us; the launch traced here: 86.1 us
  blocking collectives  46.1 us (53%)
  other arithmetic  17.8 us (21%)
  matrix products  14.6 us (17%)
  starting transfers between devices  6.48 us (7%)
  local copies, waits for them, and re-layouts  0.87 us (1%)
    all_gather x1, blocking collectives, shards(): gathered = lax.all_gather(key_value, ('rows', 'cols'), axis=0, tiled=True)  46.1 us
    dot_general x4, matrix products, project(): jnp.einsum('ikc,ch->hik', pair_normed, pair_proj, preferred_element_type=...  12.6 us
    reduce_sum x5, other arithmetic, normalize(): variance = jnp.mean(centered * centered, axis=-1, keepdims=True)  9.52 us
    reduce_sum x5, other arithmetic, normalize(): average = jnp.mean(matrix, axis=-1, keepdims=True)  6.56 us
    all_to_all x1, starting transfers between devices, shards(): lax.all_to_all(bias_tile, 'cols', split_axis=1, concat_axis=2, tiled=True)  6.48 us
  transfers between devices with their start and end apart: 1, of which 0 were waited for; matrix products, arithmetic and copies ran while one was open for 3% of the time, Pallas kernels for 0%

commit v1 on v0

v1 whole, which is shorter than its diff:
```python
import functools

import jax
import jax.numpy as jnp
from jax import lax
from jax.experimental import pallas as pl
from jax.experimental.pallas import tpu as pltpu
from jax.sharding import PartitionSpec as P

MESH = pl.DeviceIdType.MESH
F32, BF16 = jnp.float32, jnp.bfloat16


def normalize(matrix):
    average = jnp.mean(matrix, axis=-1, keepdims=True)
    centered = matrix - average
    variance = jnp.mean(centered * centered, axis=-1, keepdims=True)
    return centered * lax.rsqrt(variance + 1e-05)


def nt(a, b):
    return lax.dot_general(a, b, (((1,), (1,)), ((), ())), preferred_element_type=F32)


def kernel(
    nr, nc, chunks, group,
    singles, pair, chain, wproj, qbias, pproj, oproj, out,
    pair_v, w_v, o_v, rowbuf, keybuf, bias_s, q_s, k_s, v_s, part, recv,
    pair_sem, w_sem, row_send, row_recv, key_send, key_recv, out_send, out_recv,
):
    own, feats = singles.shape
    tile_rows, tile_cols, chans = pair.shape
    heads = pproj.shape[1]
    dim = feats // heads
    me_p, me_r, me_c = lax.axis_index("parts"), lax.axis_index("rows"), lax.axis_index("cols")
    flat = me_r * nc + me_c
    step = tile_rows // chunks

    def pair_copy(k):
        rows = pl.ds(k * step, step)
        return pltpu.make_async_copy(pair.at[rows], pair_v.at[rows], pair_sem.at[k])

    w_copy = pltpu.make_async_copy(wproj, w_v, w_sem.at[0])
    o_copy = pltpu.make_async_copy(oproj, o_v, w_sem.at[1])
    pair_copy(0).start()
    barrier = pltpu.get_barrier_semaphore()

    def greet(k, carry):
        other = lax.rem(flat + k, nr * nc)
        pl.semaphore_signal(
            barrier, inc=1, device_id=(me_p, other // nc, lax.rem(other, nc)), device_id_type=MESH
        )
        return carry

    lax.fori_loop(1, nr * nc, greet, 0)
    for k in range(1, chunks):
        pair_copy(k).start()
    w_copy.start()
    o_copy.start()

    wt = pproj[...].astype(F32).T.astype(BF16)

    def bias_chunk(k):
        pair_copy(k).wait()

        def body(g, carry):
            for u in range(group):
                i = k * step + g * group + u
                x = normalize(pair_v[i].astype(F32)).astype(BF16)
                bias_s[pl.ds(pl.multiple_of(i * heads, heads), heads), :] = nt(wt, x).astype(BF16)
            return carry

        lax.fori_loop(0, step // group, body, 0)

    bias_chunk(0)
    pl.semaphore_wait(barrier, nr * nc - 1)

    def row_copy(d):
        return pltpu.make_async_remote_copy(
            src_ref=singles, dst_ref=rowbuf.at[me_c],
            send_sem=row_send.at[d], recv_sem=row_recv.at[me_c],
            device_id=(me_p, me_r, lax.rem(me_c + d, nc)), device_id_type=MESH,
        )

    key_home = flat // nr
    key_slot = lax.rem(flat, nr)

    def key_copy(d):
        return pltpu.make_async_remote_copy(
            src_ref=singles, dst_ref=keybuf.at[key_slot],
            send_sem=key_send.at[d], recv_sem=key_recv.at[key_slot],
            device_id=(me_p, lax.rem(me_r + d, nr), key_home), device_id_type=MESH,
        )

    for d in range(1, nr):
        key_copy(d).start()

    @pl.when(key_home != me_c)
    def _():
        key_copy(0).start()

    for d in range(1, nc):
        row_copy(d).start()

    mine = singles[...]
    rowbuf[me_c] = mine

    @pl.when(key_home == me_c)
    def _():
        keybuf[key_slot] = mine

    for k in range(1, chunks):
        bias_chunk(k)

    w_copy.wait()
    o_copy.wait()
    normed = normalize(mine.astype(F32)).astype(BF16)
    gate_in = jnp.dot(normed, w_v[:, 3 * feats :], preferred_element_type=F32)
    gating = 1.0 / (1.0 + jnp.exp(-gate_in))

    for k in range(nr):
        @pl.when(me_c * nr + k != flat)
        def _():
            pltpu.make_async_remote_copy(
                src_ref=singles, dst_ref=keybuf.at[k],
                send_sem=key_send.at[0], recv_sem=key_recv.at[k],
                device_id=(me_p, me_r, lax.rem(me_c + 1, nc)), device_id_type=MESH,
            ).wait_recv()

    keys_in = keybuf[...].astype(F32).reshape(nr * own, feats)
    kn = normalize(keys_in).astype(BF16)
    kv = jnp.dot(kn, w_v[:, feats : 3 * feats], preferred_element_type=F32)
    k_s[...] = kv[:, :feats].astype(BF16)
    v_s[...] = kv[:, feats:].astype(BF16)

    def row_arrival(s):
        return pltpu.make_async_remote_copy(
            src_ref=singles, dst_ref=rowbuf.at[s],
            send_sem=row_send.at[0], recv_sem=row_recv.at[s],
            device_id=(me_p, me_r, lax.rem(me_c + 1, nc)), device_id_type=MESH,
        )

    for d in range(1, nc):
        row_arrival(lax.rem(me_c + d, nc)).wait_recv()
    rows_in = rowbuf[...].astype(F32).reshape(nc * own, feats)
    rn = normalize(rows_in).astype(BF16)
    q = jnp.dot(rn, w_v[:, :feats], preferred_element_type=F32) + qbias[...]
    q_s[...] = q.astype(BF16).astype(F32)

    live = chain[0]
    for k in range(1, chain.shape[0] - 1):
        live = live + chain[k]
    keys_at = lax.broadcasted_iota(jnp.int32, (1, tile_cols), 1) + me_c * tile_cols
    key_live = keys_at < live
    head_at = lax.broadcasted_iota(jnp.int32, (heads, feats), 0)
    feat_at = lax.broadcasted_iota(jnp.int32, (heads, feats), 1)
    block = (feat_at >= head_at * dim) & (feat_at < (head_at + 1) * dim)
    stat_head = lax.broadcasted_iota(jnp.int32, (heads, 128), 0)
    stat_lane = lax.broadcasted_iota(jnp.int32, (heads, 128), 1)
    scale = dim ** (-0.5)

    def attend(b, dst):
        qb = q_s[pl.ds(pl.multiple_of(b * own, own), own), :]
        qd = jnp.where(block[None], qb[:, None, :], 0.0).reshape(own * heads, feats).astype(BF16)
        bias = bias_s[pl.ds(pl.multiple_of(b * own * heads, own * heads), own * heads), :]
        s = nt(qd, k_s[...]) * scale + bias.astype(F32)
        s = jnp.where(key_live, s, -1e30)
        m = jnp.max(s, axis=-1, keepdims=True)
        p = jnp.exp(s - m)
        l = jnp.sum(p, axis=-1, keepdims=True)
        n = jnp.dot(p.astype(BF16), v_s[...], preferred_element_type=F32)
        n = jnp.sum(jnp.where(block[None], n.reshape(own, heads, feats), 0.0), axis=1)
        m3 = m.reshape(own, heads, 1)
        l3 = l.reshape(own, heads, 1)
        st = jnp.where((stat_lane == stat_head)[None], m3, 0.0)
        st = jnp.where((stat_lane == stat_head + 64)[None], l3, st)
        dst[:, :feats] = n
        dst[:, feats:] = jnp.sum(st, axis=1)

    def out_copy(d):
        to = lax.rem(me_c + d, nc)
        return pltpu.make_async_remote_copy(
            src_ref=part.at[to], dst_ref=recv.at[me_c],
            send_sem=out_send.at[d], recv_sem=out_recv.at[me_c],
            device_id=(me_p, me_r, to), device_id_type=MESH,
        )

    def remote_block(d, carry):
        to = lax.rem(me_c + d, nc)
        attend(to, part.at[to])
        out_copy(d).start()
        return carry

    lax.fori_loop(1, nc, remote_block, 0)
    attend(me_c, recv.at[me_c])

    for d in range(1, nc):
        s = lax.rem(me_c + d, nc)
        pltpu.make_async_remote_copy(
            src_ref=part.at[s], dst_ref=recv.at[s],
            send_sem=out_send.at[d], recv_sem=out_recv.at[s],
            device_id=(me_p, me_r, s), device_id_type=MESH,
        ).wait_recv()

    stats = recv[:, :, feats:]
    lanes = lax.broadcasted_iota(jnp.int32, (1, 1, 128), 2)
    top = jnp.max(stats, axis=0, keepdims=True)
    a = jnp.exp(stats - top)
    total = jnp.sum(a * pltpu.roll(stats, 64, 2), axis=0, keepdims=True)
    coef = jnp.where(lanes < heads, a / total, 0.0).reshape(nc * own, 128)
    eh = lax.broadcasted_iota(jnp.int32, (128, feats), 0)
    ef = lax.broadcasted_iota(jnp.int32, (128, feats), 1)
    expand = ((ef >= eh * dim) & (ef < (eh + 1) * dim)).astype(F32)
    wide = jnp.dot(coef, expand, precision=lax.Precision.HIGHEST, preferred_element_type=F32)
    averaged = jnp.sum(recv[:, :, :feats] * wide.reshape(nc, own, feats), axis=0)
    attended = (gating * averaged).astype(BF16)
    out[...] = jnp.dot(attended, o_v[...], preferred_element_type=F32).astype(out.dtype)

    for d in range(1, nr):
        key_copy(d).wait_send()

    @pl.when(key_home != me_c)
    def _():
        key_copy(0).wait_send()

    for d in range(1, nc):
        row_copy(d).wait_send()
        out_copy(d).wait_send()


def shards(nr, nc, singles, pair, chain_sizes, single_proj, query_bias, pair_proj, out_proj):
    own, feats = singles.shape
    tile_rows, tile_cols, chans = pair.shape
    heads = pair_proj.shape[1]
    chunks = 8
    vmem = pl.BlockSpec(memory_space=pltpu.VMEM)
    smem = pl.BlockSpec(memory_space=pltpu.SMEM)
    hbm = pl.BlockSpec(memory_space=pl.ANY)
    dma = pltpu.SemaphoreType.DMA
    return pl.pallas_call(
        functools.partial(kernel, nr, nc, chunks, 4),
        out_shape=jax.ShapeDtypeStruct((own, feats), BF16),
        in_specs=[vmem, hbm, smem, hbm, vmem, vmem, hbm],
        out_specs=vmem,
        scratch_shapes=[
            pltpu.VMEM(pair.shape, BF16),
            pltpu.VMEM(single_proj.shape, BF16),
            pltpu.VMEM(out_proj.shape, BF16),
            pltpu.VMEM((nc, own, feats), BF16),
            pltpu.VMEM((nr, own, feats), BF16),
            pltpu.VMEM((tile_rows * heads, tile_cols), BF16),
            pltpu.VMEM((tile_rows, feats), F32),
            pltpu.VMEM((tile_cols, feats), BF16),
            pltpu.VMEM((tile_cols, feats), BF16),
            pltpu.VMEM((nc, own, feats + 128), F32),
            pltpu.VMEM((nc, own, feats + 128), F32),
            dma((chunks,)), dma((2,)),
            dma((nc,)), dma((nc,)), dma((nr,)), dma((nr,)), dma((nc,)), dma((nc,)),
        ],
        compiler_params=pltpu.CompilerParams(
            collective_id=0, has_side_effects=True, vmem_limit_bytes=50 * 1024 * 1024
        ),
        name="pair_attention",
    )(singles, pair, chain_sizes, single_proj, query_bias.reshape(1, feats), pair_proj, out_proj)


def solution(mesh):
    placed = (
        P(("parts", "rows", "cols"), None),
        P(("parts", "rows"), "cols", None),
        P("parts"),
        P(),
        P(),
        P(),
        P(),
    )
    return jax.shard_map(
        functools.partial(shards, mesh.shape["rows"], mesh.shape["cols"]),
        mesh=mesh,
        in_specs=placed,
        out_specs=P(("parts", "rows", "cols"), None),
        check_vma=False,
    )
```

time: 86.6 us -> 33 us (0.38)
  blocking collectives: 46.1 us -> 0 us
  Pallas kernels: 0 us -> 26.9 us
  other arithmetic: 17.8 us -> 0 us
  matrix products: 14.6 us -> 0 us
  starting transfers between devices: 6.48 us -> 0 us
  local copies, waits for them, and re-layouts: 0.87 us -> 5.72 us
    all_gather x1 -> x0, blocking collectives: 46.1 us -> none  [shards(): gathered = lax.all_gather(key_value, ('rows', 'cols'), axis=0, tiled=True)]
    pallas_call x0 -> x1, Pallas kernels: none -> 26.9 us  [shards(): pl.pallas_call(functools.partial(kernel, nr, nc, chunks, 4), out_shape=ja...]
    reduce_sum x12 -> x0, other arithmetic: 17.1 us -> none  [the longest x5 9.52 us: normalize(): variance = jnp.mean(centered * centered, axis=-1, keepdims=True)]
    dot_general x8 -> x0, matrix products: 14.6 us -> none  [the longest x4 12.6 us: project(): jnp.einsum('ikc,ch->hik', pair_normed, pair_proj, preferred_element_type=...]
    all_to_all x1 -> x0, starting transfers between devices: 6.48 us -> none  [shards(): lax.all_to_all(bias_tile, 'cols', split_axis=1, concat_axis=2, tiled=True)]
    unnamed x10, local copies, waits for them, and re-layouts: 0.02 us -> 5.04 us
  transfers between devices with their start and end apart: 1 -> 0, of which waited for: 0 -> 0; matrix products, arithmetic and copies ran while one was open for 3% -> 0% of each run, Pallas kernels for 0% -> 0%
where the time goes in v1:
time: 33 us; the launch traced here: 32.7 us
  Pallas kernels  26.9 us (82%)
  local copies, waits for them, and re-layouts  5.72 us (17%)
    pallas_call x1, Pallas kernels, shards(): pl.pallas_call(functools.partial(kernel, nr, nc, chunks, 4), out_shape=ja...  26.9 us
    unnamed x10, local copies, waits for them, and re-layouts  5.04 us
    reshape x1, local copies, waits for them, and re-layouts, shards(): query_bias.reshape(1, feats)  0.68 us

profile of v1, /device:TPU:0, one launch (start us, length us, event | category | flops | bytes accessed | tf_op | source)
XLA Modules:
  0.0 32.7 jit_solution(995426419464619105)
XLA Ops:
  0.0 0.7 %reshape.3.qbias = f32[1,384]{1,0:T(1,128)S(1)} reshape(f32[384]{0:T(512)} %param.11) | data formatting | bytes 3072 | tf_op jit(solution)/shard_map/reshape | solution.py:264
  0.7 0.8 %copy.8.pproj = bf16[128,16]{1,0:T(8,128)(2,1)S(1)} copy(bf16[128,16]{0,1:T(8,128)(2,1)} %param.12) | data formatting | bytes 8192 | tf_op args[5]
  1.5 0.0 copy-start
  1.5 1.3 %copy-done = bf16[384,1536]{1,0:T(8,128)(2,1)S(1)} copy-done((bf16[384,1536]{1,0:T(8,128)(2,1)S(1)}, bf16[384,1536]{1,0:T(8,128)(2,1)}, u32[]{:S(2)}) %copy-start) | copy-done | bytes 1179672
  2.8 0.0 copy-start.1
  2.8 1.0 %copy-done.1 = bf16[384,384]{1,0:T(8,128)(2,1)S(1)} copy-done((bf16[384,384]{1,0:T(8,128)(2,1)S(1)}, bf16[384,384]{1,0:T(8,128)(2,1)}, u32[]{:S(2)}) %copy-start.1) | copy-done | bytes 294936
  3.7 0.0 copy-start.2
  3.7 0.7 %copy-done.2 = bf16[32,384]{1,0:T(8,128)(2,1)S(1)} copy-done((bf16[32,384]{1,0:T(8,128)(2,1)S(1)}, bf16[32,384]{1,0:T(8,128)(2,1)}, u32[]{:S(2)}) %copy-start.2) | copy-done | bytes 24600
  4.5 0.0 copy-start.3
  4.5 0.7 %copy-done.3 = s32[8]{0:T(128)S(1)} copy-done((s32[8]{0:T(128)S(1)}, s32[8]{0:T(128)}, u32[]{:S(2)}) %copy-start.3) | copy-done | bytes 56
  5.1 26.9 %pair_attention.1 = bf16[32,384]{1,0:T(8,128)(2,1)S(1)} custom-call(bf16[32,384]{1,0:T(8,128)(2,1)S(1)} %copy-done.2, bf16[128,128,128]{2,1,0:T(8,128)(2,1)} %pair.1, s32[8]{0:T(128)S(1)} %copy-done.3, bf16[384,1536]{1,0:T(8,128)(2,1)S(1)} %copy-done, f32[1,384]{1,0:T(1,128)S(1)} %reshape.3.qbias, bf16[128,16]{1,0:T(8,128)(2,1)S(1)} %copy.8.pproj, ...), custom_call_target="tpu_custom_call" | custom-call | tf_op jit(solution)/shard_map/pair_attention/pallas_call | solution.py:240
  32.1 0.6 %copy.10 = bf16[32,384]{1,0:T(8,128)(2,1)} copy(bf16[32,384]{1,0:T(8,128)(2,1)S(1)} %pair_attention.1) | data formatting | bytes 49152
Async XLA Ops:
  1.5 1.3 %copy-start = (bf16[384,1536]{1,0:T(8,128)(2,1)S(1)}, bf16[384,1536]{1,0:T(8,128)(2,1)}, u32[]{:S(2)}) copy-start(bf16[384,1536]{1,0:T(8,128)(2,1)} %wproj.1) | copy-start | bytes 3538948
  2.8 1.0 %copy-start.1 = (bf16[384,384]{1,0:T(8,128)(2,1)S(1)}, bf16[384,384]{1,0:T(8,128)(2,1)}, u32[]{:S(2)}) copy-start(bf16[384,384]{1,0:T(8,128)(2,1)} %oproj.1) | copy-start | bytes 884740
  3.7 0.7 %copy-start.2 = (bf16[32,384]{1,0:T(8,128)(2,1)S(1)}, bf16[32,384]{1,0:T(8,128)(2,1)}, u32[]{:S(2)}) copy-start(bf16[32,384]{1,0:T(8,128)(2,1)} %singles.1) | copy-start | bytes 73732
  4.5 0.7 %copy-start.3 = (s32[8]{0:T(128)S(1)}, s32[8]{0:T(128)}, u32[]{:S(2)}) copy-start(s32[8]{0:T(128)} %chain.1) | copy-start | bytes 100

commit v2 on v1

--- a/solution.py
+++ b/solution.py
@@ -24,13 +24,14 @@
 
 def kernel(
     nr, nc, chunks, group,
-    singles, pair, chain, wproj, qbias, pproj, oproj, out,
-    pair_v, w_v, o_v, rowbuf, keybuf, bias_s, q_s, k_s, v_s, part, recv,
-    pair_sem, w_sem, row_send, row_recv, key_send, key_recv, out_send, out_recv,
+    singles_h, pair, chain_h, wproj, qbias_h, pproj_h, oproj, out,
+    singles, chain, qbias, pproj, pair_v, w_v, o_v, rowbuf, keybuf, bias_s, q_s, k_s, v_s, wide_s, norm_s,
+    part, part_stat, recv, recv_stat, pair_sem, w_sem,
+    row_send, row_recv, key_send, key_recv, out_send, out_recv, stat_send, stat_recv,
 ):
     own, feats = singles.shape
     tile_rows, tile_cols, chans = pair.shape
-    heads = pproj.shape[1]
+    heads = pproj.shape[0]
     dim = feats // heads
     me_p, me_r, me_c = lax.axis_index("parts"), lax.axis_index("rows"), lax.axis_index("cols")
     flat = me_r * nc + me_c
@@ -42,6 +43,14 @@
 
     w_copy = pltpu.make_async_copy(wproj, w_v, w_sem.at[0])
     o_copy = pltpu.make_async_copy(oproj, o_v, w_sem.at[1])
+    small = [
+        pltpu.make_async_copy(src, dst, w_sem.at[2 + n])
+        for n, (src, dst) in enumerate(
+            ((singles_h, singles), (pproj_h, pproj), (chain_h, chain), (qbias_h, qbias))
+        )
+    ]
+    small[0].start()
+    small[1].start()
     pair_copy(0).start()
     barrier = pltpu.get_barrier_semaphore()
 
@@ -56,21 +65,37 @@
     for k in range(1, chunks):
         pair_copy(k).start()
     w_copy.start()
+    small[2].start()
+    small[3].start()
     o_copy.start()
 
-    wt = pproj[...].astype(F32).T.astype(BF16)
+    small[0].wait()
+    small[1].wait()
+    wt = pproj[...]
+    tall = jnp.concatenate([wt] * step, axis=0)
+    tall_at = lax.broadcasted_iota(jnp.int32, tall.shape, 0)
+    for u in range(step):
+        inside = (tall_at >= u * heads) & (tall_at < (u + 1) * heads)
+        wide_s[:, u * chans : (u + 1) * chans] = jnp.where(inside, tall, 0).astype(BF16)
 
     def bias_chunk(k):
         pair_copy(k).wait()
 
         def body(g, carry):
             for u in range(group):
-                i = k * step + g * group + u
-                x = normalize(pair_v[i].astype(F32)).astype(BF16)
-                bias_s[pl.ds(pl.multiple_of(i * heads, heads), heads), :] = nt(wt, x).astype(BF16)
+                i = g * group + u
+                x = pair_v[k * step + i].astype(F32)
+                x = normalize(x).astype(BF16)
+                lanes_at = pl.ds(pl.multiple_of(i * chans, chans), chans)
+                norm_s[pl.ds(k * tile_cols, tile_cols), lanes_at] = x
             return carry
 
         lax.fori_loop(0, step // group, body, 0)
+
+    def bias_project(k):
+        rows = norm_s[pl.ds(k * tile_cols, tile_cols), :]
+        size = step * heads
+        bias_s[pl.ds(k * size, size), :] = nt(rows, wide_s[...]).T.astype(BF16)
 
     bias_chunk(0)
     pl.semaphore_wait(barrier, nr * nc - 1)
@@ -109,11 +134,23 @@
     def _():
         keybuf[key_slot] = mine
 
-    for k in range(1, chunks):
+    def later_chunk(k, carry):
         bias_chunk(k)
+        return carry
+
+    lax.fori_loop(1, chunks, later_chunk, 0)
+
+    def project_pair(k, carry):
+        bias_project(2 * k)
+        bias_project(2 * k + 1)
+        return carry
+
+    lax.fori_loop(0, chunks // 2, project_pair, 0)
 
     w_copy.wait()
     o_copy.wait()
+    small[2].wait()
+    small[3].wait()
     normed = normalize(mine.astype(F32)).astype(BF16)
     gate_in = jnp.dot(normed, w_v[:, 3 * feats :], preferred_element_type=F32)
     gating = 1.0 / (1.0 + jnp.exp(-gate_in))
@@ -131,7 +168,9 @@
     kn = normalize(keys_in).astype(BF16)
     kv = jnp.dot(kn, w_v[:, feats : 3 * feats], preferred_element_type=F32)
     k_s[...] = kv[:, :feats].astype(BF16)
-    v_s[...] = kv[:, feats:].astype(BF16)
+    values = kv[:, feats:].astype(BF16)
+    v_s[:tile_cols, :] = values
+    v_s[tile_cols:, :] = values
 
     def row_arrival(s):
         return pltpu.make_async_remote_copy(
@@ -144,7 +183,7 @@
         row_arrival(lax.rem(me_c + d, nc)).wait_recv()
     rows_in = rowbuf[...].astype(F32).reshape(nc * own, feats)
     rn = normalize(rows_in).astype(BF16)
-    q = jnp.dot(rn, w_v[:, :feats], preferred_element_type=F32) + qbias[...]
+    q = jnp.dot(rn, w_v[:, :feats], preferred_element_type=F32) + qbias[...].reshape(1, feats)
     q_s[...] = q.astype(BF16).astype(F32)
 
     live = chain[0]
@@ -159,7 +198,7 @@
     stat_lane = lax.broadcasted_iota(jnp.int32, (heads, 128), 1)
     scale = dim ** (-0.5)
 
-    def attend(b, dst):
+    def attend(b, dst, dst_stat):
         qb = q_s[pl.ds(pl.multiple_of(b * own, own), own), :]
         qd = jnp.where(block[None], qb[:, None, :], 0.0).reshape(own * heads, feats).astype(BF16)
         bias = bias_s[pl.ds(pl.multiple_of(b * own * heads, own * heads), own * heads), :]
@@ -168,41 +207,47 @@
         m = jnp.max(s, axis=-1, keepdims=True)
         p = jnp.exp(s - m)
         l = jnp.sum(p, axis=-1, keepdims=True)
-        n = jnp.dot(p.astype(BF16), v_s[...], preferred_element_type=F32)
+        high = p.astype(BF16)
+        low = (p - high.astype(F32)).astype(BF16)
+        p = jnp.concatenate([high, low], axis=1)
+        n = jnp.dot(p, v_s[...], preferred_element_type=F32)
         n = jnp.sum(jnp.where(block[None], n.reshape(own, heads, feats), 0.0), axis=1)
         m3 = m.reshape(own, heads, 1)
         l3 = l.reshape(own, heads, 1)
         st = jnp.where((stat_lane == stat_head)[None], m3, 0.0)
         st = jnp.where((stat_lane == stat_head + 64)[None], l3, st)
-        dst[:, :feats] = n
-        dst[:, feats:] = jnp.sum(st, axis=1)
-
-    def out_copy(d):
+        dst[...] = n.astype(BF16)
+        dst_stat[...] = jnp.sum(st, axis=1)
+
+    def out_copies(d, slot):
         to = lax.rem(me_c + d, nc)
-        return pltpu.make_async_remote_copy(
-            src_ref=part.at[to], dst_ref=recv.at[me_c],
-            send_sem=out_send.at[d], recv_sem=out_recv.at[me_c],
-            device_id=(me_p, me_r, to), device_id_type=MESH,
-        )
+        return [
+            pltpu.make_async_remote_copy(
+                src_ref=src.at[to], dst_ref=dst.at[slot],
+                send_sem=send.at[d], recv_sem=arrive.at[slot],
+                device_id=(me_p, me_r, to), device_id_type=MESH,
+            )
+            for src, dst, send, arrive in (
+                (part, recv, out_send, out_recv),
+                (part_stat, recv_stat, stat_send, stat_recv),
+            )
+        ]
 
     def remote_block(d, carry):
         to = lax.rem(me_c + d, nc)
-        attend(to, part.at[to])
-        out_copy(d).start()
+        attend(to, part.at[to], part_stat.at[to])
+        for copy in out_copies(d, me_c):
+            copy.start()
         return carry
 
     lax.fori_loop(1, nc, remote_block, 0)
-    attend(me_c, recv.at[me_c])
+    attend(me_c, recv.at[me_c], recv_stat.at[me_c])
 
     for d in range(1, nc):
-        s = lax.rem(me_c + d, nc)
-        pltpu.make_async_remote_copy(
-            src_ref=part.at[s], dst_ref=recv.at[s],
-            send_sem=out_send.at[d], recv_sem=out_recv.at[s],
-            device_id=(me_p, me_r, s), device_id_type=MESH,
-        ).wait_recv()
-
-    stats = recv[:, :, feats:]
+        for copy in out_copies(d, lax.rem(me_c + d, nc)):
+            copy.wait_recv()
+
+    stats = recv_stat[...]
     lanes = lax.broadcasted_iota(jnp.int32, (1, 1, 128), 2)
     top = jnp.max(stats, axis=0, keepdims=True)
     a = jnp.exp(stats - top)
@@ -212,7 +257,7 @@
     ef = lax.broadcasted_iota(jnp.int32, (128, feats), 1)
     expand = ((ef >= eh * dim) & (ef < (eh + 1) * dim)).astype(F32)
     wide = jnp.dot(coef, expand, precision=lax.Precision.HIGHEST, preferred_element_type=F32)
-    averaged = jnp.sum(recv[:, :, :feats] * wide.reshape(nc, own, feats), axis=0)
+    averaged = jnp.sum(recv[...].astype(F32) * wide.reshape(nc, own, feats), axis=0)
     attended = (gating * averaged).astype(BF16)
     out[...] = jnp.dot(attended, o_v[...], preferred_element_type=F32).astype(out.dtype)
 
@@ -225,7 +270,8 @@
 
     for d in range(1, nc):
         row_copy(d).wait_send()
-        out_copy(d).wait_send()
+        for copy in out_copies(d, me_c):
+            copy.wait_send()
 
 
 def shards(nr, nc, singles, pair, chain_sizes, single_proj, query_bias, pair_proj, out_proj):
@@ -234,15 +280,18 @@
     heads = pair_proj.shape[1]
     chunks = 8
     vmem = pl.BlockSpec(memory_space=pltpu.VMEM)
-    smem = pl.BlockSpec(memory_space=pltpu.SMEM)
-    hbm = pl.BlockSpec(memory_space=pl.ANY)
+    hbm = pl.BlockSpec(memory_space=pltpu.HBM)
     dma = pltpu.SemaphoreType.DMA
     return pl.pallas_call(
         functools.partial(kernel, nr, nc, chunks, 4),
         out_shape=jax.ShapeDtypeStruct((own, feats), BF16),
-        in_specs=[vmem, hbm, smem, hbm, vmem, vmem, hbm],
+        in_specs=[hbm] * 7,
         out_specs=vmem,
         scratch_shapes=[
+            pltpu.VMEM(singles.shape, BF16),
+            pltpu.SMEM(chain_sizes.shape, jnp.int32),
+            pltpu.VMEM(query_bias.shape, F32),
+            pltpu.VMEM((heads, chans), BF16),
             pltpu.VMEM(pair.shape, BF16),
             pltpu.VMEM(single_proj.shape, BF16),
             pltpu.VMEM(out_proj.shape, BF16),
@@ -251,17 +300,22 @@
             pltpu.VMEM((tile_rows * heads, tile_cols), BF16),
             pltpu.VMEM((tile_rows, feats), F32),
             pltpu.VMEM((tile_cols, feats), BF16),
-            pltpu.VMEM((tile_cols, feats), BF16),
-            pltpu.VMEM((nc, own, feats + 128), F32),
-            pltpu.VMEM((nc, own, feats + 128), F32),
-            dma((chunks,)), dma((2,)),
-            dma((nc,)), dma((nc,)), dma((nr,)), dma((nr,)), dma((nc,)), dma((nc,)),
+            pltpu.VMEM((2 * tile_cols, feats), BF16),
+            pltpu.VMEM((tile_rows // chunks * heads, tile_rows // chunks * chans), BF16),
+            pltpu.VMEM((chunks * tile_cols, tile_rows // chunks * chans), BF16),
+            pltpu.VMEM((nc, own, feats), BF16),
+            pltpu.VMEM((nc, own, 128), F32),
+            pltpu.VMEM((nc, own, feats), BF16),
+            pltpu.VMEM((nc, own, 128), F32),
+            dma((chunks,)), dma((6,)),
+            dma((nc,)), dma((nc,)), dma((nr,)), dma((nr,)),
+            dma((nc,)), dma((nc,)), dma((nc,)), dma((nc,)),
         ],
         compiler_params=pltpu.CompilerParams(
-            collective_id=0, has_side_effects=True, vmem_limit_bytes=50 * 1024 * 1024
+            collective_id=0, has_side_effects=True
         ),
         name="pair_attention",
-    )(singles, pair, chain_sizes, single_proj, query_bias.reshape(1, feats), pair_proj, out_proj)
+    )(singles, pair, chain_sizes, single_proj, query_bias, pair_proj.T, out_proj)
 
 
 def solution(mesh):

time: 33 us -> 25.9 us (0.78)
  local copies, waits for them, and re-layouts: 5.72 us -> 1.35 us
  Pallas kernels: 26.9 us -> 24.3 us
    unnamed x10 -> x1, local copies, waits for them, and re-layouts: 5.04 us -> 1.35 us
    pallas_call x1, Pallas kernels: 26.9 us -> 24.3 us  [shards(): pl.pallas_call(functools.partial(kernel, nr, nc, chunks, 4), out_shape=ja...]
    reshape x1 -> x0, local copies, waits for them, and re-layouts: 0.68 us -> none  [shards(): query_bias.reshape(1, feats)]
where the time goes in v2:
time: 25.9 us; the launch traced here: 25.7 us
  Pallas kernels  24.3 us (94%)
  local copies, waits for them, and re-layouts  1.35 us (5%)
    pallas_call x1, Pallas kernels, shards(): pl.pallas_call(functools.partial(kernel, nr, nc, chunks, 4), out_shape=ja...  24.3 us
    unnamed x1, local copies, waits for them, and re-layouts  1.35 us

profile of v2, /device:TPU:0, one launch (start us, length us, event | category | flops | bytes accessed | tf_op | source)
XLA Modules:
  0.0 25.7 jit_solution(2950614322177937346)
XLA Ops:
  0.0 24.3 %pair_attention.1 = bf16[32,384]{1,0:T(8,128)(2,1)} custom-call(bf16[32,384]{1,0:T(8,128)(2,1)} %singles_h.1, bf16[128,128,128]{2,1,0:T(8,128)(2,1)} %pair.1, s32[8]{0:T(128)} %chain_h.1, bf16[384,1536]{1,0:T(8,128)(2,1)} %wproj.1, f32[384]{0:T(512)} %qbias_h.1, bf16[16,128]{1,0:T(8,128)(2,1)} %bitcast.1, bf16[384,384]{1,0:T(8,128)(2,1)} %oproj.1), custom_call_target="tpu_custom_call" | custom-call | tf_op jit(solution)/shard_map/pair_attention/pallas_call | solution.py:285
  24.3 1.3 %copy.9 = bf16[32,384]{1,0:T(8,128)(2,1)} copy(bf16[32,384]{1,0:T(8,128)(2,1)} %pair_attention.1) | data formatting | bytes 49152

commit v3 on v2

--- a/solution.py
+++ b/solution.py
@@ -92,12 +92,23 @@
 
         lax.fori_loop(0, step // group, body, 0)
 
-    def bias_project(k):
-        rows = norm_s[pl.ds(k * tile_cols, tile_cols), :]
+    batch = chunks // 2
+
+    def bias_project(g, carry):
+        rows = norm_s[pl.ds(g * batch * tile_cols, batch * tile_cols), :]
         size = step * heads
-        bias_s[pl.ds(k * size, size), :] = nt(rows, wide_s[...]).T.astype(BF16)
-
-    bias_chunk(0)
+        wide_bias = nt(rows, wide_s[...])
+        for u in range(batch):
+            piece = wide_bias[u * tile_cols : (u + 1) * tile_cols, :]
+            bias_s[pl.ds((g * batch + u) * size, size), :] = piece.T.astype(BF16)
+        return carry
+
+    def later_chunk(k, carry):
+        bias_chunk(k)
+        return carry
+
+    early = min(3, chunks)
+    lax.fori_loop(0, early, later_chunk, 0)
     pl.semaphore_wait(barrier, nr * nc - 1)
 
     def row_copy(d):
@@ -134,18 +145,9 @@
     def _():
         keybuf[key_slot] = mine
 
-    def later_chunk(k, carry):
-        bias_chunk(k)
-        return carry
-
-    lax.fori_loop(1, chunks, later_chunk, 0)
-
-    def project_pair(k, carry):
-        bias_project(2 * k)
-        bias_project(2 * k + 1)
-        return carry
-
-    lax.fori_loop(0, chunks // 2, project_pair, 0)
+    lax.fori_loop(early, chunks, later_chunk, 0)
+
+    lax.fori_loop(0, chunks // batch, bias_project, 0)
 
     w_copy.wait()
     o_copy.wait()

time: 25.9 us -> 23.7 us (0.915)
  Pallas kernels: 24.3 us -> 22.1 us
    pallas_call x1, Pallas kernels: 24.3 us -> 22.1 us  [shards(): pl.pallas_call(functools.partial(kernel, nr, nc, chunks, 4), out_shape=ja...]
where the time goes in v3:
time: 23.7 us; the launch traced here: 23.5 us
  Pallas kernels  22.1 us (93%)
  local copies, waits for them, and re-layouts  1.35 us (6%)
    pallas_call x1, Pallas kernels, shards(): pl.pallas_call(functools.partial(kernel, nr, nc, chunks, 4), out_shape=ja...  22.1 us
    unnamed x1, local copies, waits for them, and re-layouts  1.35 us

profile of v3, /device:TPU:0, one launch (start us, length us, event | category | flops | bytes accessed | tf_op | source)
XLA Modules:
  0.0 23.5 jit_solution(18285257158988220153)
XLA Ops:
  0.0 22.1 %pair_attention.1 = bf16[32,384]{1,0:T(8,128)(2,1)} custom-call(bf16[32,384]{1,0:T(8,128)(2,1)} %singles_h.1, bf16[128,128,128]{2,1,0:T(8,128)(2,1)} %pair.1, s32[8]{0:T(128)} %chain_h.1, bf16[384,1536]{1,0:T(8,128)(2,1)} %wproj.1, f32[384]{0:T(512)} %qbias_h.1, bf16[16,128]{1,0:T(8,128)(2,1)} %bitcast.1, bf16[384,384]{1,0:T(8,128)(2,1)} %oproj.1), custom_call_target="tpu_custom_call" | custom-call | tf_op jit(solution)/shard_map/pair_attention/pallas_call | solution.py:287
  22.1 1.3 %copy.9 = bf16[32,384]{1,0:T(8,128)(2,1)} copy(bf16[32,384]{1,0:T(8,128)(2,1)} %pair_attention.1) | data formatting | bytes 49152
